TPU v7x, 32 devices: a whole 2x2x4 slice. The times are simulated.
32 devices in a mesh: fsdp: 2 (over core), width: 4 (over y, x), unit: 4 (over z).
Axes of the slice: x: 2, y: 2, z: 4, core: 2. Of those that a mesh axis runs over, the one named last changes fastest.
Arguments:
- train_gate: bfloat16 [8192, 8192], P(('unit', 'fsdp'), 'width'), parts along dimension 0, may hold values from -0.125 to 0.125
- low_gate: bfloat16 [8192, 32], P(('unit', 'fsdp')), parts along dimension 0, may hold values from -0.125 to 0.125
- high_gate: bfloat16 [128, 8192], P('unit', 'width'), parts along dimension 0, may hold values from -1 to 1
- train_up: bfloat16 [8192, 8192], P(('unit', 'fsdp'), 'width'), parts along dimension 0, may hold values from -0.125 to 0.125
- low_up: bfloat16 [8192, 32], P(('unit', 'fsdp')), parts along dimension 0, may hold values from -0.125 to 0.125
- high_up: bfloat16 [128, 8192], P('unit', 'width'), parts along dimension 0, may hold values from -1 to 1
- norm_train: float32 [8192], P(('unit', 'fsdp', 'width')), parts along dimension 0, may hold values from 0.25 to 1.75
- norm_step: float32 [8192], P(('unit', 'fsdp', 'width')), parts along dimension 0, may hold values from -0.3 to 0.3
Outputs:
- final_gate: bfloat16 [32768, 2048], P(('unit', 'width')), parts along dimension 0
- final_up: bfloat16 [32768, 2048], P(('unit', 'width')), parts along dimension 0
- serve_norm: bfloat16 [8192], P('unit'), parts along dimension 0
There are 4 independent parts, one for each index of `unit`. A program takes and returns all parts, laid end to end along the dimension named above; each array names one. Nothing has to cross between parts.
All inputs are finite; a program needn't handle non-finite values.
Results may differ from a plain program's by a relative error of at most 0.001.
Values may be sent and summed in bfloat16 or wider, within the bound.
A program may use at most 128 MiB of HBM per device.

v0:
```python
import jax
import jax.numpy as jnp
from jax import lax
from jax.sharding import PartitionSpec as P

mix_rate = 2.0


def body(train_gate, low_gate, high_gate, train_up, low_up, high_up, norm_train, norm_step):
    result_gate = train_gate.astype(jnp.float32) + mix_rate * jnp.dot(
        low_gate, high_gate, preferred_element_type=jnp.float32
    )
    result_up = train_up.astype(jnp.float32) + mix_rate * jnp.dot(
        low_up, high_up, preferred_element_type=jnp.float32
    )
    narrow_gate, narrow_up = (result_gate.astype(jnp.bfloat16), result_up.astype(jnp.bfloat16))
    final_gate, final_up = (
        lax.all_gather(narrow_gate, "fsdp", axis=0, tiled=True),
        lax.all_gather(narrow_up, "fsdp", axis=0, tiled=True),
    )
    final_gate, final_up = (final_gate.T, final_up.T)
    serve_norm = lax.all_gather(
        (norm_train + norm_step).astype(jnp.bfloat16), ("fsdp", "width"), axis=0, tiled=True
    )
    return (final_gate, final_up, serve_norm)


def solution(mesh):
    return jax.shard_map(
        body,
        mesh=mesh,
        in_specs=(
            P(("unit", "fsdp"), "width"),
            P(("unit", "fsdp"), None),
            P("unit", "width"),
            P(("unit", "fsdp"), "width"),
            P(("unit", "fsdp"), None),
            P("unit", "width"),
            P(("unit", "fsdp", "width")),
            P(("unit", "fsdp", "width")),
        ),
        out_specs=(P(("unit", "width"), None), P(("unit", "width"), None), P("unit")),
        check_vma=False,
    )
```

profile of v0, /device:TPU:0, one launch (start us, length us, event | category | flops | bytes accessed | tf_op | source)
XLA Modules:
  0.0 78.0 jit_solution(2958209487717878340)
XLA Ops:
  7.2 0.0 copy-start
  7.2 0.0 copy-start.2
  7.2 0.0 copy-start.1
  7.2 0.0 all-gather.4.cloned.1.call-start
  7.2 0.8 %copy-done = bf16[32,2048]{1,0:T(8,128)(2,1)S(1)} copy-done((bf16[32,2048]{1,0:T(8,128)(2,1)S(1)}, bf16[32,2048]{1,0:T(8,128)(2,1)}, u32[]{:S(2)}) %copy-start) | copy-done | bytes 131096
  8.1 5.5 %add_convert_fusion.1 = bf16[1024,2048]{1,0:T(8,128)(2,1)} fusion(bf16[1024,2048]{1,0:T(8,128)(2,1)} %param.8, bf16[1024,32]{0,1:T(8,128)(2,1)} %param.9, bf16[32,2048]{1,0:T(8,128)(2,1)S(1)} %copy-done), kind=kOutput, calls=%fused_computation.1 | convolution fusion | flops 142606336 | bytes 8585216 | tf_op jit(solution)/shard_map/dot_general | solution.py:10
  13.6 0.0 copy-start.3
  13.6 0.0 copy-start.4
  13.6 0.0 all-gather.4.cloned.1.call-update
  13.6 0.0 all-gather.6.cloned.1.call-start
  13.7 0.0 copy-done.2
  13.7 0.0 copy-done.1
  13.7 5.4 %add_convert_fusion = bf16[1024,2048]{1,0:T(8,128)(2,1)} fusion(bf16[1024,2048]{1,0:T(8,128)(2,1)} %param.11, bf16[1024,32]{0,1:T(8,128)(2,1)S(1)} %copy-done.2, bf16[32,2048]{1,0:T(8,128)(2,1)S(1)} %copy-done.1), kind=kOutput, calls=%fused_computation | convolution fusion | flops 142606336 | bytes 8585216 | tf_op jit(solution)/shard_map/dot_general | solution.py:13
  19.1 0.0 all-gather.6.cloned.1.call-update
  19.1 0.0 copy-done.3
  19.1 0.0 copy-done.4
  19.2 14.9 %all-gather = bf16[8,1,256]{2,1,0:T(2,128)(2,1)S(1)} all-gather(bf16[1,1,256]{2,1,0:T(2,128)(2,1)S(1)} %reshape.6), channel_id=1, replica_groups=mesh['fsdp'=2,'width'=4,'unit'=4] {'fsdp','width'}, dimensions={0}, use_global_device_ids=true | all-gather | bytes 4608 | tf_op jit(solution)/shard_map/all_gather | solution.py:22
  34.1 0.6 copy.17
  34.7 1.7 %all-gather.4.cloned.1.call-done = bf16[2048,2048]{1,0:T(8,128)(2,1)} async-done(((bf16[1024,2048]{1,0:T(8,128)(2,1)}), bf16[2048,2048]{1,0:T(8,128)(2,1)}) %all-gather.4.cloned.1.call-update) | async-done | bytes 8388624 | tf_op jit(solution)/shard_map/all_gather | solution.py:18
  36.4 12.3 %copy.15 = bf16[2048,2048]{1,0:T(8,128)(2,1)} copy(bf16[2048,2048]{0,1:T(8,128)(2,1)} %bitcast.8) | data formatting | bytes 16777216
  48.7 10.3 %all-gather.6.cloned.1.call-done = bf16[2048,2048]{1,0:T(8,128)(2,1)} async-done(((bf16[1024,2048]{1,0:T(8,128)(2,1)}), bf16[2048,2048]{1,0:T(8,128)(2,1)}) %all-gather.6.cloned.1.call-update) | async-done | bytes 8388624 | tf_op jit(solution)/shard_map/all_gather | solution.py:19
  58.9 12.2 %copy.16 = bf16[2048,2048]{1,0:T(8,128)(2,1)} copy(bf16[2048,2048]{0,1:T(8,128)(2,1)} %bitcast.9) | data formatting | bytes 16777216
  (3 shorter events, 0.0 us)
Async XLA Ops:
  7.2 0.9 %copy-start = (bf16[32,2048]{1,0:T(8,128)(2,1)S(1)}, bf16[32,2048]{1,0:T(8,128)(2,1)}, u32[]{:S(2)}) copy-start(bf16[32,2048]{1,0:T(8,128)(2,1)} %param.10) | copy-start | bytes 393220
  7.2 6.5 %copy-start.2 = (bf16[1024,32]{0,1:T(8,128)(2,1)S(1)}, bf16[1024,32]{0,1:T(8,128)(2,1)}, u32[]{:S(2)}) copy-start(bf16[1024,32]{0,1:T(8,128)(2,1)} %param.12) | copy-start | bytes 196612
  7.2 6.5 %copy-start.1 = (bf16[32,2048]{1,0:T(8,128)(2,1)S(1)}, bf16[32,2048]{1,0:T(8,128)(2,1)}, u32[]{:S(2)}) copy-start(bf16[32,2048]{1,0:T(8,128)(2,1)} %param.13) | copy-start | bytes 393220
  7.2 29.1 %all-gather.4.cloned.1.call-start = ((), (), s32[]{:S(2)}) async-start(), calls=%async_computation | async-start | bytes 12582912 | tf_op jit(solution)/shard_map/all_gather | solution.py:18
  13.6 5.5 %copy-start.3 = (f32[256]{0:T(256)S(1)}, f32[256]{0:T(256)}, u32[]{:S(2)}) copy-start(f32[256]{0:T(256)} %param.14) | copy-start | bytes 3076
  13.6 5.5 %copy-start.4 = (f32[256]{0:T(256)S(1)}, f32[256]{0:T(256)}, u32[]{:S(2)}) copy-start(f32[256]{0:T(256)} %param.15) | copy-start | bytes 3076
  13.6 45.3 %all-gather.6.cloned.1.call-start = ((), (), s32[]{:S(2)}) async-start(), calls=%async_computation.1 | async-start | bytes 12582912 | tf_op jit(solution)/shard_map/all_gather | solution.py:19
Sparse Core Ops, SparseCore 0:
  13.7 22.5 all-gather.3
  37.9 21.0 all-gather.5
where the time goes:
time: 78.8 us; the launch traced here: 78 us
  local copies, waits for them, and re-layouts  26 us (33%)
  blocking collectives  14.9 us (19%)
  between operations  14.1 us (18%)
  waiting for transfers between devices  12 us (15%)
  matrix products  10.9 us (14%)
    unnamed x14, local copies, waits for them, and re-layouts  26 us
    all_gather x1, blocking collectives, body(): lax.all_gather((norm_train + norm_step).astype(jnp.bfloat16), ('fsdp', 'w...  14.9 us
    all_gather x1, waiting for transfers between devices, body(): lax.all_gather(narrow_up, 'fsdp', axis=0, tiled=True)  10.3 us
    dot_general x1, matrix products, body(): jnp.dot(low_gate, high_gate, preferred_element_type=jnp.float32)  5.52 us
    dot_general x1, matrix products, body(): jnp.dot(low_up, high_up, preferred_element_type=jnp.float32)  5.41 us
    all_gather x1, waiting for transfers between devices, body(): lax.all_gather(narrow_gate, 'fsdp', axis=0, tiled=True)  1.67 us
  transfers between devices with their start and end apart: 2, of which 2 were waited for; matrix products, arithmetic and copies ran while one was open for 24% of the time, Pallas kernels for 0%

commit v1 on v0

--- a/solution.py
+++ b/solution.py
@@ -19,9 +19,23 @@
         lax.all_gather(narrow_up, "fsdp", axis=0, tiled=True),
     )
     final_gate, final_up = (final_gate.T, final_up.T)
-    serve_norm = lax.all_gather(
-        (norm_train + norm_step).astype(jnp.bfloat16), ("fsdp", "width"), axis=0, tiled=True
-    )
+
+    def _supply_strips_all(original, at_axis):
+        lane_axis = ("fsdp", "width")
+        side_arr = lax.axis_size(lane_axis)
+        t1 = lax.axis_index(lane_axis)
+        part_next, r2 = (side_arr, t1)
+        block_out, now = (original, 1)
+        while now < part_next:
+            opened = list(map(lambda dev_i: (dev_i, dev_i ^ now), range(part_next)))
+            v_now = lax.ppermute(block_out, lane_axis, perm=opened)
+            parts_out = jnp.concatenate([block_out, v_now], at_axis)
+            outer = jnp.concatenate([v_now, block_out], at_axis)
+            block_out = jnp.where(r2 & now == 0, parts_out, outer)
+            now = 2 * now
+        return block_out
+
+    serve_norm = _supply_strips_all((norm_train + norm_step).astype(jnp.bfloat16), 0)
     return (final_gate, final_up, serve_norm)
 
 

time: 78.8 us -> 78.8 us (level)
  blocking collectives: 14.9 us -> 0 us
  waiting for transfers between devices: 12 us -> 21.7 us
  starting transfers between devices: 0.08 us -> 5.28 us
    all_gather x1 -> x0, blocking collectives: 14.9 us -> none  [body(): lax.all_gather((norm_train + norm_step).astype(jnp.bfloat16), ('fsdp', 'w...]
    all_gather x1, waiting for transfers between devices: 1.67 us -> 7.11 us  [body(): lax.all_gather(narrow_gate, 'fsdp', axis=0, tiled=True)]
    ppermute x0 -> x3, starting transfers between devices: none -> 5.2 us  [_supply_strips_all(): v_now = lax.ppermute(block_out, lane_axis, perm=opened)]
    ppermute x0 -> x3, waiting for transfers between devices: none -> 4.25 us  [_supply_strips_all(): v_now = lax.ppermute(block_out, lane_axis, perm=opened)]
    unnamed x14 -> x12, local copies, waits for them, and re-layouts: 26 us -> 25.4 us
  transfers between devices with their start and end apart: 2 -> 5, of which waited for: 2 -> 5; matrix products, arithmetic and copies ran while one was open for 24% -> 24% of each run, Pallas kernels for 0% -> 0%
where the time goes in v1:
time: 78.8 us; the launch traced here: 78 us
  local copies, waits for them, and re-layouts  25.4 us (32%)
  waiting for transfers between devices  21.7 us (28%)
  between operations  14.1 us (18%)
  matrix products  10.9 us (14%)
  starting transfers between devices  5.28 us (7%)
    unnamed x12, local copies, waits for them, and re-layouts  25.4 us
    all_gather x1, waiting for transfers between devices, body(): lax.all_gather(narrow_up, 'fsdp', axis=0, tiled=True)  10.3 us
    all_gather x1, waiting for transfers between devices, body(): lax.all_gather(narrow_gate, 'fsdp', axis=0, tiled=True)  7.11 us
    dot_general x1, matrix products, body(): jnp.dot(low_gate, high_gate, preferred_element_type=jnp.float32)  5.52 us
    dot_general x1, matrix products, body(): jnp.dot(low_up, high_up, preferred_element_type=jnp.float32)  5.41 us
    ppermute x3, starting transfers between devices, _supply_strips_all(): v_now = lax.ppermute(block_out, lane_axis, perm=opened)  5.2 us
    ppermute x3, waiting for transfers between devices, _supply_strips_all(): v_now = lax.ppermute(block_out, lane_axis, perm=opened)  4.25 us
  transfers between devices with their start and end apart: 5, of which 5 were waited for; matrix products, arithmetic and copies ran while one was open for 24% of the time, Pallas kernels for 0%

profile of v1, /device:TPU:0, one launch (start us, length us, event | category | flops | bytes accessed | tf_op | source)
XLA Modules:
  0.0 78.0 jit_solution(7873092715766185569)
XLA Ops:
  7.2 0.0 copy-start
  7.2 0.0 copy-start.2
  7.2 0.0 all-gather.3.cloned.1.call-start
  7.2 0.8 %copy-done = bf16[32,2048]{1,0:T(8,128)(2,1)S(1)} copy-done((bf16[32,2048]{1,0:T(8,128)(2,1)S(1)}, bf16[32,2048]{1,0:T(8,128)(2,1)}, u32[]{:S(2)}) %copy-start) | copy-done | bytes 131096
  8.1 5.5 %add_convert_fusion.1 = bf16[1024,2048]{1,0:T(8,128)(2,1)} fusion(bf16[1024,2048]{1,0:T(8,128)(2,1)} %param.8, bf16[1024,32]{0,1:T(8,128)(2,1)} %param.9, bf16[32,2048]{1,0:T(8,128)(2,1)S(1)} %copy-done), kind=kOutput, calls=%fused_computation.1 | convolution fusion | flops 142606336 | bytes 8585216 | tf_op jit(solution)/shard_map/dot_general | solution.py:10
  13.6 0.0 all-gather.3.cloned.1.call-update
  13.6 0.0 all-gather.5.cloned.1.call-start
  13.7 0.0 copy-done.2
  13.7 0.0 copy-done.1
  13.7 5.4 %add_convert_fusion = bf16[1024,2048]{1,0:T(8,128)(2,1)} fusion(bf16[1024,2048]{1,0:T(8,128)(2,1)} %param.11, bf16[1024,32]{0,1:T(8,128)(2,1)S(1)} %copy-done.2, bf16[32,2048]{1,0:T(8,128)(2,1)S(1)} %copy-done.1), kind=kOutput, calls=%fused_computation | convolution fusion | flops 142606336 | bytes 8585216 | tf_op jit(solution)/shard_map/dot_general | solution.py:13
  19.1 0.0 all-gather.5.cloned.1.call-update
  19.1 0.0 copy-done.3
  19.1 0.0 copy-done.4
  19.2 3.0 %collective-permute-start = (bf16[256]{0:T(256)(128)(2,1)S(1)}, bf16[256]{0:T(256)(128)(2,1)S(1)}, u32[]{:S(2)}, u32[]{:S(2)}) collective-permute-start(bf16[256]{0:T(256)(128)(2,1)S(1)} %add_convert_fusion.2), channel_id=1, source_target_pairs={{0,4},{4,0},{8,12},{12,8},{16,20},{20,16},{24,28},{28,24},{1,5},{5... | collective-permute-start | bytes 1544 | tf_op jit(solution)/shard_map/ppermute | solution.py:31
  22.2 1.5 %collective-permute-done = bf16[256]{0:T(256)(128)(2,1)S(1)} collective-permute-done((bf16[256]{0:T(256)(128)(2,1)S(1)}, bf16[256]{0:T(256)(128)(2,1)S(1)}, u32[]{:S(2)}, u32[]{:S(2)}) %collective-permute-start) | collective-permute-done | bytes 544 | tf_op jit(solution)/shard_map/ppermute | solution.py:31
  23.8 2.1 %collective-permute-start.1 = (bf16[512]{0:T(512)(128)(2,1)S(1)}, bf16[512]{0:T(512)(128)(2,1)S(1)}, u32[]{:S(2)}, u32[]{:S(2)}) collective-permute-start(bf16[512]{0:T(512)(128)(2,1)S(1)} %maximum_select_fusion.2), channel_id=1, source_target_pairs={{0,8},{4,12},{8,0},{12,4},{16,24},{20,28},{24,16},{28,20},{1,9},{5... | collective-permute-start | bytes 3080 | tf_op jit(solution)/shard_map/ppermute | solution.py:31
  25.9 1.6 %collective-permute-done.1 = bf16[512]{0:T(512)(128)(2,1)S(1)} collective-permute-done((bf16[512]{0:T(512)(128)(2,1)S(1)}, bf16[512]{0:T(512)(128)(2,1)S(1)}, u32[]{:S(2)}, u32[]{:S(2)}) %collective-permute-start.1) | collective-permute-done | bytes 1056 | tf_op jit(solution)/shard_map/ppermute | solution.py:31
  27.4 0.1 collective-permute-start.2
  27.5 1.1 %collective-permute-done.2 = bf16[1024]{0:T(1024)(128)(2,1)S(1)} collective-permute-done((bf16[1024]{0:T(1024)(128)(2,1)S(1)}, bf16[1024]{0:T(1024)(128)(2,1)S(1)}, u32[]{:S(2)}, u32[]{:S(2)}) %collective-permute-start.2) | collective-permute-done | bytes 2080 | tf_op jit(solution)/shard_map/ppermute | solution.py:31
  28.6 0.6 maximum_select_fusion
  29.2 7.1 %all-gather.3.cloned.1.call-done = bf16[2048,2048]{1,0:T(8,128)(2,1)} async-done(((bf16[1024,2048]{1,0:T(8,128)(2,1)}), bf16[2048,2048]{1,0:T(8,128)(2,1)}) %all-gather.3.cloned.1.call-update) | async-done | bytes 8388624 | tf_op jit(solution)/shard_map/all_gather | solution.py:18
  36.4 12.3 %copy.11 = bf16[2048,2048]{1,0:T(8,128)(2,1)} copy(bf16[2048,2048]{0,1:T(8,128)(2,1)} %bitcast.6) | data formatting | bytes 16777216
  48.7 10.3 %all-gather.5.cloned.1.call-done = bf16[2048,2048]{1,0:T(8,128)(2,1)} async-done(((bf16[1024,2048]{1,0:T(8,128)(2,1)}), bf16[2048,2048]{1,0:T(8,128)(2,1)}) %all-gather.5.cloned.1.call-update) | async-done | bytes 8388624 | tf_op jit(solution)/shard_map/all_gather | solution.py:19
  58.9 12.2 %copy.12 = bf16[2048,2048]{1,0:T(8,128)(2,1)} copy(bf16[2048,2048]{0,1:T(8,128)(2,1)} %bitcast.7) | data formatting | bytes 16777216
  (6 shorter events, 0.0 us)
Async XLA Ops:
  7.2 0.9 %copy-start = (bf16[32,2048]{1,0:T(8,128)(2,1)S(1)}, bf16[32,2048]{1,0:T(8,128)(2,1)}, u32[]{:S(2)}) copy-start(bf16[32,2048]{1,0:T(8,128)(2,1)} %param.10) | copy-start | bytes 393220
  7.2 6.5 %copy-start.2 = (bf16[1024,32]{0,1:T(8,128)(2,1)S(1)}, bf16[1024,32]{0,1:T(8,128)(2,1)}, u32[]{:S(2)}) copy-start(bf16[1024,32]{0,1:T(8,128)(2,1)} %param.12) | copy-start | bytes 196612
  7.2 6.5 %copy-start.1 = (bf16[32,2048]{1,0:T(8,128)(2,1)S(1)}, bf16[32,2048]{1,0:T(8,128)(2,1)}, u32[]{:S(2)}) copy-start(bf16[32,2048]{1,0:T(8,128)(2,1)} %param.13) | copy-start | bytes 393220
  7.2 29.1 %all-gather.3.cloned.1.call-start = ((), (), s32[]{:S(2)}) async-start(), calls=%async_computation | async-start | bytes 12582912 | tf_op jit(solution)/shard_map/all_gather | solution.py:18
  13.6 5.5 %copy-start.3 = (f32[256]{0:T(256)S(1)}, f32[256]{0:T(256)}, u32[]{:S(2)}) copy-start(f32[256]{0:T(256)} %param.14) | copy-start | bytes 3076
  13.6 5.5 %copy-start.4 = (f32[256]{0:T(256)S(1)}, f32[256]{0:T(256)}, u32[]{:S(2)}) copy-start(f32[256]{0:T(256)} %param.15) | copy-start | bytes 3076
  13.6 45.3 %all-gather.5.cloned.1.call-start = ((), (), s32[]{:S(2)}) async-start(), calls=%async_computation.1 | async-start | bytes 12582912 | tf_op jit(solution)/shard_map/all_gather | solution.py:19
  19.2 4.6 %collective-permute-start = (bf16[256]{0:T(256)(128)(2,1)S(1)}, bf16[256]{0:T(256)(128)(2,1)S(1)}, u32[]{:S(2)}, u32[]{:S(2)}) collective-permute-start(bf16[256]{0:T(256)(128)(2,1)S(1)} %add_convert_fusion.2), channel_id=1, source_target_pairs={{0,4},{4,0},{8,12},{12,8},{16,20},{20,16},{24,28},{28,24},{1,5},{5... | collective-permute-start | bytes 1544 | tf_op jit(solution)/shard_map/ppermute | solution.py:31
  23.8 3.7 %collective-permute-start.1 = (bf16[512]{0:T(512)(128)(2,1)S(1)}, bf16[512]{0:T(512)(128)(2,1)S(1)}, u32[]{:S(2)}, u32[]{:S(2)}) collective-permute-start(bf16[512]{0:T(512)(128)(2,1)S(1)} %maximum_select_fusion.2), channel_id=1, source_target_pairs={{0,8},{4,12},{8,0},{12,4},{16,24},{20,28},{24,16},{28,20},{1,9},{5... | collective-permute-start | bytes 3080 | tf_op jit(solution)/shard_map/ppermute | solution.py:31
  27.4 1.2 %collective-permute-start.2 = (bf16[1024]{0:T(1024)(128)(2,1)S(1)}, bf16[1024]{0:T(1024)(128)(2,1)S(1)}, u32[]{:S(2)}, u32[]{:S(2)}) collective-permute-start(bf16[1024]{0:T(1024)(128)(2,1)S(1)} %maximum_select_fusion.1), channel_id=1, source_target_pairs={{0,16},{4,20},{8,24},{12,28},{16,0},{20,4},{24,8},{28,12},{1,17},{... | collective-permute-start | bytes 6152 | tf_op jit(solution)/shard_map/ppermute | solution.py:31
Sparse Core Ops, SparseCore 0:
  13.7 22.5 all-gather.2
  37.9 21.0 all-gather.4
